TPU v7x, 32 devices: a whole 2x2x4 slice. The times are simulated.
32 devices in a mesh: dp: 8 (over z, x), cand: 4 (over y, core).
Axes of the slice: x: 2, y: 2, z: 4, core: 2. Of those that a mesh axis runs over, the one named last changes fastest.
Arguments:
- hidden: bfloat16 [16, 32, 128, 768], P('dp', 'cand'), may hold values from -24 to 24
- attn_weight: bfloat16 [768, 3072], P('dp'), may hold values from -1 to 1
- norm_gain: float32 [768], replicated, may hold values from 0.2 to 4
- pos_bias: float32 [12, 128, 128], replicated, may hold values from -5 to 5
- score_weight: float32 [768], replicated, may hold values from -4 to 4
- pair_lengths: int32 [16, 32], P('dp', 'cand'), may hold values from 32 to 128
- labels: int32 [16, 32], P('dp', 'cand'), may hold values from 0 to 3
Outputs:
- update: float32 [768, 3072], P('dp')
- loss: float32 [16], P('dp')
All inputs are finite; a program needn't handle non-finite values.
Results may differ from a plain program's by a relative error of at most 0.017.
Values may be sent and summed in bfloat16 or wider, within the bound.
No kernel may reach another device: no remote copies, remote signals or barrier semaphores. Data moves between devices by JAX's collectives and lax.ppermute only.
A program may use at most 128 MiB of HBM per device.

v0:
```python
import jax
import jax.numpy as jnp
from jax import lax
from jax.sharding import PartitionSpec as P

EPS = 1e-06


def rms_rows(values, gain):
    factor = lax.rsqrt(jnp.mean(values * values, axis=-1, keepdims=True) + EPS)
    return values * factor * gain


def attend(qkv, pos_bias, pair_len):
    batch, seq, triple = qkv.shape
    width = triple // 3
    heads = pos_bias.shape[0]
    head_size = width // heads
    parts = qkv.reshape(batch, seq, 3, heads, head_size)
    logits = jnp.einsum(
        "bqhd,bkhd->bhqk", parts[:, :, 0], parts[:, :, 1], preferred_element_type=jnp.float32
    )
    logits = logits + pos_bias[None]
    valid = jnp.arange(seq, dtype=jnp.int32)[None, :] < pair_len[:, None]
    logits = jnp.where(valid[:, None, None, :], logits, -1e30)
    highest = jnp.max(logits, axis=-1, keepdims=True)
    expo = jnp.exp(logits - highest)
    probs = (expo / jnp.sum(expo, axis=-1, keepdims=True)).astype(jnp.bfloat16)
    context = jnp.einsum(
        "bhqk,bkhd->bqhd", probs, parts[:, :, 2], preferred_element_type=jnp.float32
    )
    return context.astype(jnp.bfloat16).reshape(batch, seq, width)


def score_head(pooled, score_weight):
    return jnp.sum(rms_rows(pooled, 1.0) * score_weight, axis=-1)


def shards(hidden, attn_weight, norm_gain, pos_bias, score_weight, pair_lengths, labels):
    q_local, c_local, seq, width = hidden.shape
    weights = lax.all_gather(attn_weight, "dp", axis=0, tiled=True)
    tokens = hidden.reshape(q_local * c_local, seq, width)
    pair_len = pair_lengths.reshape(-1)
    values = tokens.astype(jnp.float32)
    normed = rms_rows(values, norm_gain).astype(jnp.bfloat16)
    flat_norm = normed.reshape(-1, width)
    qkv = jnp.dot(flat_norm, weights[:, : 3 * width], preferred_element_type=jnp.float32)
    qkv = qkv.astype(jnp.bfloat16).reshape(q_local * c_local, seq, 3 * width)
    context, attend_back = jax.vjp(lambda block: attend(block, pos_bias, pair_len), qkv)
    flat_ctx = context.reshape(-1, width)
    out_rows = values + jnp.dot(
        flat_ctx, weights[:, 3 * width :], preferred_element_type=jnp.float32
    ).reshape(values.shape)
    live = (jnp.arange(seq, dtype=jnp.int32)[None, :] < pair_len[:, None]).astype(jnp.float32)
    share = live / pair_len.astype(jnp.float32)[:, None]
    pooled = jnp.sum(out_rows * share[:, :, None], axis=1)
    flat_scores, head_back = jax.vjp(lambda vector: score_head(vector, score_weight), pooled)
    scores = flat_scores.reshape(q_local, c_local)
    target = jnp.exp(labels.astype(jnp.float32))
    highest = lax.pmax(jnp.max(scores, axis=1), "cand")
    expsum, target_sum, target_dot = lax.psum(
        (
            jnp.sum(jnp.exp(scores - highest[:, None]), axis=1),
            jnp.sum(target, axis=1),
            jnp.sum(target * scores, axis=1),
        ),
        "cand",
    )
    loss = highest + jnp.log(expsum) - target_dot / target_sum
    score_grad = jnp.exp(scores - highest[:, None]) / expsum[:, None] - target / target_sum[:, None]
    pooled_grad = head_back(score_grad.reshape(-1))[0]
    out_grad = (pooled_grad[:, None, :] * share[:, :, None]).astype(jnp.bfloat16)
    flat_out = out_grad.reshape(-1, width)
    context_grad = jnp.dot(flat_out, weights[:, 3 * width :].T, preferred_element_type=jnp.float32)
    context_grad = context_grad.astype(jnp.bfloat16).reshape(context.shape)
    qkv_grad = attend_back(context_grad)[0].reshape(-1, 3 * width)
    dims = (((0,), (0,)), ((), ()))
    first = lax.dot_general(flat_norm, qkv_grad, dims, preferred_element_type=jnp.float32)
    second = lax.dot_general(flat_ctx, flat_out, dims, preferred_element_type=jnp.float32)
    shard = lax.psum_scatter(
        jnp.concatenate([first, second], axis=1).astype(jnp.bfloat16),
        "dp",
        scatter_dimension=0,
        tiled=True,
    ).astype(jnp.float32)
    shard = lax.psum(shard.astype(jnp.bfloat16), "cand").astype(jnp.float32)
    squares = lax.psum(jnp.sum(shard * shard), "dp")
    rms_value = jnp.sqrt(squares / (4.0 * width * width))
    update = shard / (rms_value + EPS)
    return (update, loss)


def solution(mesh):
    in_specs = (
        P("dp", "cand", None, None),
        P("dp", None),
        P(),
        P(),
        P(),
        P("dp", "cand"),
        P("dp", "cand"),
    )
    out_specs = (P("dp", None), P("dp"))
    return jax.shard_map(shards, mesh=mesh, in_specs=in_specs, out_specs=out_specs, check_vma=False)
```

profile of v0, /device:TPU:0, one launch (start us, length us, event | category | flops | bytes accessed | tf_op | source)
XLA Modules:
  0.0 460.7 jit_solution(10536083495842605806)
XLA Ops:
  18.8 73.4 %all-gather.2.cloned.1.call-done = bf16[768,3072]{1,0:T(8,128)(2,1)} async-done(((bf16[96,3072]{1,0:T(8,128)(2,1)}), bf16[768,3072]{1,0:T(8,128)(2,1)}) %all-gather.2.cloned.1.call-update) | async-done | bytes 4718608 | tf_op jit(solution)/shard_map/all_gather | solution.py:41
  92.3 12.5 %convolution_convert_fusion = bf16[2048,2304]{1,0:T(8,128)(2,1)} fusion(bf16[2048,768]{1,0:T(8,128)(2,1)} %fusion.13, bf16[768,3072]{1,0:T(8,128)(2,1)} %all-gather.2.cloned.1.call-done), kind=kOutput, calls=%fused_computation.11 | convolution fusion | flops 7252475904 | bytes 16121856 | tf_op jit(solution)/shard_map/dot_general | solution.py:47
  104.8 12.7 %copy.20 = bf16[2048,2304]{0,1:T(8,128)(2,1)} copy(bf16[2048,2304]{1,0:T(8,128)(2,1)} %convolution_convert_fusion) | data formatting | bytes 18874368 | tf_op jit(solution)/shard_map/convert_element_type | solution.py:48
  117.5 10.9 %copy.45 = bf16[288,8,16,128]{3,2,1,0:T(8,128)(2,1)} copy(bf16[288,8,16,128]{3,1,2,0:T(8,128)(2,1)} %bitcast.104) | data formatting | bytes 18874368
  128.4 6.4 %fusion.56 = (bf16[16,128,1,12,64]{1,0,4,3,2:T(8,128)(2,1)}, bf16[16,128,1,12,64]{1,0,4,3,2:T(8,128)(2,1)}, bf16[16,128,1,12,64]{1,0,4,3,2:T(8,128)(2,1)S(1)}) fusion(bf16[16,128,3,12,64]{1,0,4,3,2:T(8,128)(2,1)} %bitcast.103), kind=kLoop, calls=%fused_computation.91 | loop fusion | bytes 18874368 | tf_op jit(solution)/shard_map/jvp()/slice | solution.py:30
  134.8 7.5 %fusion.5 = (f32[16,12,128]{2,1,0:T(8,128)S(1)}, f32[16,12,128,128]{2,3,1,0:T(8,128)S(1)}) fusion(f32[12,128,128]{1,2,0:T(8,128)S(1)} %copy-done.11, pred[16,128]{1,0:T(8,128)(4,1)S(1)} %iota_compare_fusion, bf16[16,128,1,12,64]{1,0,4,3,2:T(8,128)(2,1)S(1)} %get-tuple-element.15, bf16[16,128,1,12,64]{1,0,4,3,2:T(8,128)(2,1)} %get-tuple-element.14), kind=kOutput, calls=%fused_computation.13 | convolution fusion | flops 412065792 | bytes 19761152 | tf_op jit(solution)/shard_map/jvp(bqhd,bkhd->bhqk)/dot_general | solution.py:20
  142.3 3.4 fusion.37
  146.9 8.1 %convert_reduce_fusion = (f32[16,12,128]{2,1,0:T(8,128)S(1)}, pred[16,12,128,128]{2,3,1,0:T(32,128)(4,1)}, bf16[16,12,128,128]{2,3,1,0:T(8,128)(2,1)S(1)}) fusion(f32[16,12,128]{2,1,0:T(8,128)S(1)} %get-tuple-element.20, f32[16,12,128,128]{2,3,1,0:T(8,128)S(1)} %get-tuple-element.21, f32[12,128,128]{1,2,0:T(8,128)S(1)} %copy-done.11, ...), kind=kLoop, calls=%fused_computation.7 | loop fusion | flops 25141248 | bytes 23103488 | tf_op jit(solution)/shard_map/jvp()/reduce_sum | solution.py:26
  159.2 4.6 fusion.15
  164.3 5.7 %pmax.7 = f32[2]{0:T(128)S(1)} all-reduce(f32[2]{0:T(128)S(1)} %reduce_max.19), channel_id=1, replica_groups=mesh['dp'=8,'cand'=4] {'cand'}, use_global_device_ids=true, to_apply=%region_7.8 | all-reduce | flops 2 | bytes 16 | tf_op jit(solution)/shard_map/pmax | solution.py:60
  170.2 6.6 %all-reduce.3 = (f32[2]{0:T(128)S(1)}, f32[2]{0:T(128)S(1)}, f32[2]{0:T(128)S(1)}) all-reduce(f32[2]{0:T(128)S(1)} %get-tuple-element.3, f32[2]{0:T(128)S(1)} %get-tuple-element.4, f32[2]{0:T(128)S(1)} %get-tuple-element.2), channel_id=1, replica_groups=mesh['dp'=8,'cand'=4] {'cand'}, use_global_device_ids=true, to_apply=%region_11.12 | all-reduce | flops 6 | bytes 48 | tf_op jit(solution)/shard_map/psum | solution.py:61
  177.7 5.3 %convolution_convert_fusion.2 = bf16[2048,768]{1,0:T(8,128)(2,1)} fusion(bf16[2048,768]{1,0:T(8,128)(2,1)S(1)} %fusion.11, bf16[768,3072]{1,0:T(8,128)(2,1)} %all-gather.2.cloned.1.call-done), kind=kOutput, calls=%fused_computation.41 | convolution fusion | flops 2417491968 | bytes 7471104 | tf_op jit(solution)/shard_map/dot_general | solution.py:74
  182.9 4.7 %copy.27 = bf16[2048,768]{0,1:T(8,128)(2,1)} copy(bf16[2048,768]{1,0:T(8,128)(2,1)} %convolution_convert_fusion.2) | data formatting | bytes 6291456 | tf_op jit(solution)/shard_map/convert_element_type | solution.py:75
  192.2 9.0 %convert_bitcast_fusion.2 = bf16[16,128,1,12,64]{1,4,3,0,2:T(8,128)(2,1)} fusion(bf16[16,12,128,128]{2,3,1,0:T(8,128)(2,1)} %copy-done.2, bf16[16,12,64,128]{3,0,2,1:T(8,128)(2,1)S(1)} %bitcast.108), kind=kOutput, calls=%fused_computation.50 | convolution fusion | flops 404226048 | bytes 12582912 | tf_op jit(solution)/shard_map/transpose(jvp(bhqk,bkhd->bqhd))/dot_general | solution.py:29
  201.2 12.6 %fusion.3 = (f32[16,12,128]{2,1,0:T(8,128)S(1)}, bf16[16,12,128,128]{2,3,1,0:T(8,128)(2,1)}) fusion(f32[16,12,128]{2,1,0:T(8,128)S(1)} %multiply_divide_fusion, f32[16,12,128]{2,1,0:T(8,128)S(1)} %get-tuple-element.20, f32[16,12,128,128]{2,3,1,0:T(8,128)} %copy-done, f32[12,128,128]{1,2,0:T(8,128)S(1)} %copy-done.11, ...), kind=kOutput, calls=%fused_computation.5 | convolution fusion | flops 427794432 | bytes 26249216 | tf_op jit(solution)/shard_map/transpose(jvp(bhqk,bkhd->bqhd))/dot_general | solution.py:29
  213.9 10.1 %fusion.53 = (f32[16,12,128]{2,1,0:T(8,128)S(1)}, f32[16,12,128,128]{2,3,1,0:T(8,128)}) fusion(f32[16,12,128]{2,1,0:T(8,128)S(1)} %get-tuple-element.20, f32[16,12,128,128]{2,3,1,0:T(8,128)S(1)} %bitcast.102, f32[12,128,128]{1,2,0:T(8,128)S(1)} %copy-done.11, pred[16,128]{1,0:T(8,128)(4,1)S(1)} %iota_compare_fusion, f32[16,12,128]{2,1,0:T(8,128)S(1)} %neg.9, ...), kind=kLoop, calls=%fused_computation.90 | loop fusion | flops 25141248 | bytes 32638976 | tf_op jit(solution)/shard_map/transpose(jvp())/reduce_sum | solution.py:27
  224.1 11.4 %convert_bitcast_fusion.1 = bf16[16,128,1,12,64]{1,4,3,0,2:T(8,128)(2,1)} fusion(bf16[16,128,1,12,64]{1,0,4,3,2:T(8,128)(2,1)} %get-tuple-element.14, f32[16,12,128,128]{2,3,1,0:T(8,128)} %get-tuple-element.9, pred[16,12,128,128]{2,3,1,0:T(32,128)(4,1)} %get-tuple-element.11, f32[16,12,128]{2,1,0:T(8,128)S(1)} %negate_divide_fusion, ...), kind=kOutput, calls=%fused_computation.49 | convolution fusion | flops 413663232 | bytes 22120448 | tf_op jit(solution)/shard_map/transpose(jvp(bqhd,bkhd->bhqk))/dot_general | solution.py:20
  237.0 4.2 convert_bitcast_fusion
  244.2 6.8 %pad_add_fusion = bf16[16,128,3,12,64]{1,4,3,0,2:T(8,128)(2,1)} fusion(bf16[16,128,1,12,64]{1,4,3,0,2:T(8,128)(2,1)} %convert_bitcast_fusion, bf16[16,128,1,12,64]{1,4,3,0,2:T(8,128)(2,1)} %convert_bitcast_fusion.1, bf16[16,128,1,12,64]{1,4,3,0,2:T(8,128)(2,1)S(1)} %copy-done.12), kind=kLoop, calls=%fused_computation.17 | loop fusion | flops 9437184 | bytes 18874368 | tf_op jit(solution)/shard_map/transpose(jvp())/add_any | solution.py:21
  251.0 26.1 %copy.33 = bf16[16,128,3,12,64]{1,0,4,3,2:T(8,128)(2,1)} copy(bf16[16,128,3,12,64]{1,4,3,0,2:T(8,128)(2,1)} %pad_add_fusion) | data formatting | bytes 18874368 | tf_op jit(solution)/shard_map/transpose(jvp())/add_any | solution.py:21
  279.6 11.4 %fusion.22 = bf16[768,2304]{1,0:T(8,128)(2,1)S(1)} fusion(bf16[2048,768]{1,0:T(8,128)(2,1)S(1)} %bitcast.113, bf16[288,8,16,128]{3,2,1,0:T(8,128)(2,1)} %bitcast.110), kind=kOutput, calls=%fused_computation.37 | convolution fusion | flops 7249526784 | bytes 16121856 | tf_op jit(solution)/shard_map/dot_general | solution.py:78
  296.5 94.1 %reduce-scatter.2.cloned.1.call-done = bf16[96,3072]{1,0:T(8,128)(2,1)} async-done(((bf16[768,3072]{1,0:T(8,128)(2,1)}), bf16[96,3072]{1,0:T(8,128)(2,1)}) %reduce-scatter.2.cloned.1.call-update) | async-done | bytes 589840 | tf_op jit(solution)/shard_map/reduce_scatter | solution.py:80
  390.6 35.8 %all-reduce.6.cloned.1.call-done = bf16[96,3072]{1,0:T(8,128)(2,1)} async-done(((bf16[96,3072]{1,0:T(8,128)(2,1)}), bf16[96,3072]{1,0:T(8,128)(2,1)}) %all-reduce.6.cloned.1.call-update) | async-done | bytes 589840 | tf_op jit(solution)/shard_map/psum | solution.py:86
  428.9 22.0 %psum.38 = f32[]{:T(128)} all-reduce(f32[]{:T(128)} %fusion.41), channel_id=1, replica_groups=mesh['dp'=8,'cand'=4] {'dp'}, use_global_device_ids=true, to_apply=%region_19.20 | all-reduce | flops 1 | bytes 8 | tf_op jit(solution)/shard_map/psum | solution.py:87
  (84 shorter events, 40.2 us)
Async XLA Ops:
  7.2 6.8 %copy-start.5 = (bf16[2,8,128,768]{3,2,1,0:T(8,128)(2,1)S(1)}, bf16[2,8,128,768]{3,2,1,0:T(8,128)(2,1)}, u32[]{:S(2)}) copy-start(bf16[2,8,128,768]{3,2,1,0:T(8,128)(2,1)} %param.7) | copy-start | bytes 9437188
  7.2 6.8 %copy-start.17 = (f32[768]{0:T(1024)S(1)}, f32[768]{0:T(1024)}, u32[]{:S(2)}) copy-start(f32[768]{0:T(1024)} %param.9) | copy-start | bytes 9220
  7.2 85.1 %all-gather.2.cloned.1.call-start = ((), (), s32[]{:S(2)}) async-start(), calls=%async_computation.1 | async-start | bytes 5308416 | tf_op jit(solution)/shard_map/all_gather | solution.py:41
  7.9 382.7 %reduce-scatter.2.cloned.1.call-start = ((), (), s32[]{:S(2)}) async-start(), calls=%async_computation.2 | async-start | bytes 5308416 | tf_op jit(solution)/shard_map/reduce_scatter | solution.py:80
  128.4 6.4 %copy-start.11 = (f32[12,128,128]{1,2,0:T(8,128)S(1)}, f32[12,128,128]{1,2,0:T(8,128)}, u32[]{:S(2)}) copy-start(f32[12,128,128]{1,2,0:T(8,128)} %copy.24) | copy-start | bytes 2359300
  134.8 7.6 %copy-start.3 = (bf16[16,128,1,12,64]{1,0,4,3,2:T(8,128)(2,1)}, bf16[16,128,1,12,64]{1,0,4,3,2:T(8,128)(2,1)S(1)}, u32[]{:S(2)}) copy-start(bf16[16,128,1,12,64]{1,0,4,3,2:T(8,128)(2,1)S(1)} %get-tuple-element.15) | copy-start | bytes 9437188
  142.3 4.6 copy-start
  146.9 8.1 %copy-start.8 = (bf16[16,128,1,12,64]{1,0,4,3,2:T(8,128)(2,1)S(1)}, bf16[16,128,1,12,64]{1,0,4,3,2:T(8,128)(2,1)}, u32[]{:S(2)}) copy-start(bf16[16,128,1,12,64]{1,0,4,3,2:T(8,128)(2,1)} %get-tuple-element.13) | copy-start | bytes 9437188
  155.0 3.2 copy-start.2
  155.0 4.2 copy-start.6
  158.2 5.6 %copy-start.9 = (bf16[16,12,64,128]{3,2,1,0:T(8,128)(2,1)}, bf16[16,12,64,128]{3,2,1,0:T(8,128)(2,1)S(1)}, u32[]{:S(2)}) copy-start(bf16[16,12,64,128]{3,2,1,0:T(8,128)(2,1)S(1)} %fusion.36) | copy-start | bytes 9437188
  159.2 4.7 %copy-start.16 = (f32[768]{0:T(1024)S(1)}, f32[768]{0:T(1024)}, u32[]{:S(2)}) copy-start(f32[768]{0:T(1024)} %param.11) | copy-start | bytes 9220
  159.2 10.8 %copy-start.18 = (s32[2,8]{1,0:T(2,128)S(1)}, s32[2,8]{1,0:T(2,128)}, u32[]{:S(2)}) copy-start(s32[2,8]{1,0:T(2,128)} %param.13) | copy-start | bytes 196
  192.2 21.7 %slice-start = ((s8[12582912]{0:T(1024)(128)(4,1)}), s8[4194304]{0:T(1024)(128)(4,1)S(1)}, s32[]{:S(2)}) async-start(s8[12582912]{0:T(1024)(128)(4,1)} %bitcast.101), calls=%async_computation.4 | async-start | bytes 8388608
  201.2 12.7 %slice-start.1 = ((s8[12582912]{0:T(1024)(128)(4,1)}), s8[4194304]{0:T(1024)(128)(4,1)S(1)}, s32[]{:S(2)}) async-start(s8[12582912]{0:T(1024)(128)(4,1)} %bitcast.101), calls=%async_computation.5 | async-start | bytes 8388608
  201.2 12.7 %slice-start.2 = ((s8[12582912]{0:T(1024)(128)(4,1)}), s8[4194304]{0:T(1024)(128)(4,1)S(1)}, s32[]{:S(2)}) async-start(s8[12582912]{0:T(1024)(128)(4,1)} %bitcast.101), calls=%async_computation.6 | async-start | bytes 8388608
  224.1 11.4 %copy-start.1 = (f32[16,12,128,128]{2,3,1,0:T(8,128)S(1)}, f32[16,12,128,128]{2,3,1,0:T(8,128)}, u32[]{:S(2)}) copy-start(f32[16,12,128,128]{2,3,1,0:T(8,128)} %get-tuple-element.9) | copy-start | bytes 37748740
  224.1 11.8 %copy-start.4 = (bf16[16,128,1,12,64]{1,0,4,3,2:T(8,128)(2,1)S(1)}, bf16[16,128,1,12,64]{1,0,4,3,2:T(8,128)(2,1)}, u32[]{:S(2)}) copy-start(bf16[16,128,1,12,64]{1,0,4,3,2:T(8,128)(2,1)} %copy-done.3) | copy-start | bytes 9437188
  224.1 12.9 %copy-start.7 = (pred[16,12,128,128]{2,3,1,0:T(32,128)(4,1)S(1)}, pred[16,12,128,128]{2,3,1,0:T(32,128)(4,1)}, u32[]{:S(2)}) copy-start(pred[16,12,128,128]{2,3,1,0:T(32,128)(4,1)} %get-tuple-element.11) | copy-start | bytes 9437188
  241.2 3.0 copy-start.12
  251.0 26.2 %copy-start.10 = (bf16[16,12,64,128]{3,2,1,0:T(8,128)(2,1)S(1)}, bf16[16,12,64,128]{3,2,1,0:T(8,128)(2,1)}, u32[]{:S(2)}) copy-start(bf16[16,12,64,128]{3,2,1,0:T(8,128)(2,1)} %copy-done.9) | copy-start | bytes 9437188
  277.2 2.5 copy-start.15
  279.6 11.4 %copy-start.14 = (bf16[16,128,768]{2,1,0:T(8,128)(2,1)S(1)}, bf16[16,128,768]{2,1,0:T(8,128)(2,1)}, u32[]{:S(2)}) copy-start(bf16[16,128,768]{2,1,0:T(8,128)(2,1)} %multiply_convert_fusion) | copy-start | bytes 9437188
  296.5 130.0 %all-reduce.6.cloned.1.call-start = ((), (), s32[]{:S(2)}) async-start(), calls=%async_computation.3 | async-start | bytes 1179648 | tf_op jit(solution)/shard_map/psum | solution.py:86
  (1 other events, 1.6 us)
Sparse Core Ops, SparseCore 0:
  10.2 82.0 all-gather.1
  296.6 93.9 reduce-scatter.1
  393.0 33.3 all-reduce.5
where the time goes:
time: 464 us; the launch traced here: 461 us
  waiting for transfers between devices  204 us (44%)
  matrix products  83.9 us (18%)
  local copies, waits for them, and re-layouts  76.2 us (16%)
  other arithmetic  47.1 us (10%)
  blocking collectives  34.2 us (7%)
  between operations  15.2 us (3%)
    reduce_scatter x1, waiting for transfers between devices, shards(): lax.psum_scatter(jnp.concatenate([first, second], axis=1).astype(jnp.bflo...  94.1 us
    all_gather x1, waiting for transfers between devices, shards(): weights = lax.all_gather(attn_weight, 'dp', axis=0, tiled=True)  73.4 us
    psum x1, waiting for transfers between devices, shards(): shard = lax.psum(shard.astype(jnp.bfloat16), 'cand').astype(jnp.float32)  35.8 us
    add_any x1, local copies, waits for them, and re-layouts, attend(): parts[:, :, 0]  26.1 us
    dot_general x3, matrix products, attend(): jnp.einsum('bhqk,bkhd->bqhd', probs, parts[:, :, 2], preferred_element_ty...  24.4 us
    dot_general x3, matrix products, attend(): jnp.einsum('bqhd,bkhd->bhqk', parts[:, :, 0], parts[:, :, 1], preferred_e...  23.1 us
    unnamed x47, local copies, waits for them, and re-layouts  22.7 us
    psum x1, blocking collectives, shards(): squares = lax.psum(jnp.sum(shard * shard), 'dp')  22 us
  transfers between devices with their start and end apart: 3, of which 3 were waited for; matrix products, arithmetic and copies ran while one was open for 2% of the time, Pallas kernels for 0%

commit v1 on v0

v1 whole, which is shorter than its diff:
```python
import functools

import jax
import jax.numpy as jnp
from jax import lax
from jax.experimental import pallas as pl
from jax.experimental.pallas import tpu as pltpu
from jax.sharding import PartitionSpec as P

EPS = 1e-06
F32 = jnp.float32
BF16 = jnp.bfloat16
LANES = 128
NN = (((1,), (0,)), ((), ()))
NT = (((1,), (1,)), ((), ()))
TN = (((0,), (0,)), ((), ()))


def dot(a, b, dims=NN):
    return lax.dot_general(a, b, dims, preferred_element_type=F32)


def split2(x):
    high = x.astype(BF16)
    return high, (x - high.astype(F32)).astype(BF16)


def norm_kernel(step, len_ref, hid_ref, gain_ref, normed_ref, normed_t_ref, mean_ref):
    seq = hid_ref.shape[1]
    for b in range(step):
        pair_len = len_ref[pl.program_id(0) * step + b]
        x = hid_ref[b].astype(F32)
        factor = lax.rsqrt(jnp.mean(x * x, axis=-1, keepdims=True) + EPS)
        n = (x * factor * gain_ref[...]).astype(BF16)
        normed_ref[b * seq : (b + 1) * seq, :] = n
        normed_t_ref[:, b * seq : (b + 1) * seq] = n.T
        live = lax.broadcasted_iota(jnp.int32, x.shape, 0) < pair_len
        total = jnp.sum(jnp.where(live, x, 0.0), axis=0, keepdims=True)
        mean_ref[b] = total / pair_len.astype(F32)


def fwd_kernel(step, heads, len_ref, normed_ref, w_ref, bias_ref, qkv_ref, pt_ref, c_ref, ctx_ref):
    seq = bias_ref.shape[1]
    width = w_ref.shape[1] // 3
    hd = width // heads
    qkv_ref[...] = dot(normed_ref[...], w_ref[...]).astype(BF16)
    ones = jnp.ones((8, seq), BF16)
    for b in range(step):
        pair_len = len_ref[pl.program_id(0) * step + b]
        rows = slice(b * seq, (b + 1) * seq)
        key_live = lax.broadcasted_iota(jnp.int32, (seq, seq), 0) < pair_len
        query_live = lax.broadcasted_iota(jnp.int32, (1, seq), 1) < pair_len
        sums = []
        for h in range(heads):
            q = qkv_ref[rows, h * hd : (h + 1) * hd]
            k = qkv_ref[rows, width + h * hd : width + (h + 1) * hd]
            st = dot(k, q, NT) + bias_ref[h]
            st = jnp.where(key_live, st, -1e30)
            e = jnp.exp(st - jnp.max(st, axis=0, keepdims=True))
            share = jnp.where(query_live, 1.0 / jnp.sum(e, axis=0, keepdims=True), 0.0)
            pt = (e * share).astype(BF16)
            pt_ref[b, h] = pt
            sums.append(dot(ones, pt, NT)[0:1, :])
        c = jnp.concatenate(sums, axis=0)
        c_ref[b] = c
        high, low = split2(c)
        v = qkv_ref[rows, 2 * width : 3 * width]
        ctx = dot(high, v) + dot(low, v)
        col_head = lax.broadcasted_iota(jnp.int32, ctx.shape, 1) // hd
        own = col_head == lax.broadcasted_iota(jnp.int32, ctx.shape, 0)
        ctx_ref[b] = jnp.sum(jnp.where(own, ctx, 0.0), axis=0, keepdims=True)


def value_kernel(groups, heads, *refs):
    c_refs, (normed_ref, a_ref) = refs[:groups], refs[groups:]
    normed = normed_ref[...]
    for g in range(groups):
        a_ref[0, g * heads : (g + 1) * heads, :] = dot(c_refs[g][0].astype(BF16), normed)


def score_kernel(groups, *refs):
    ctx_refs = refs[:groups]
    mean_ref, len_ref, label_ref, wo_ref, sw_ref, pooled_ref, ctx_ref, out_ref = refs[groups:]
    ctx = jnp.concatenate([r[...] for r in ctx_refs], axis=1)
    ctx_ref[...] = ctx
    high, low = split2(ctx / len_ref[...])
    pooled = mean_ref[...] + dot(high, wo_ref[...]) + dot(low, wo_ref[...])
    pooled_ref[...] = pooled
    factor = lax.rsqrt(jnp.mean(pooled * pooled, axis=-1, keepdims=True) + EPS)
    scores = jnp.sum(pooled * factor * sw_ref[...], axis=-1, keepdims=True)
    lane = lax.broadcasted_iota(jnp.int32, out_ref.shape, 1)
    out_ref[...] = jnp.where(lane == 0, scores, label_ref[...])


def head_kernel(c_local, heads, all_ref, pooled_ref, ctx_ref, len_ref, a_ref, wo_ref, sw_ref,
                g_ref, dwo_ref, dwv_ref, loss_ref):
    pairs, width = pooled_ref.shape
    hd = width // heads
    every = all_ref[...]
    score, label = every[:, 0:1], every[:, 1:2]
    own_score, own_label = every[:pairs, 0:1], every[:pairs, 1:2]
    weight = jnp.exp(label)
    query = lax.rem(lax.broadcasted_iota(jnp.int32, score.shape, 0), pairs) // c_local
    own_query = lax.broadcasted_iota(jnp.int32, own_score.shape, 0) // c_local
    score_grad = jnp.zeros_like(own_score)
    lane = lax.broadcasted_iota(jnp.int32, loss_ref.shape, 1)
    losses = jnp.zeros(loss_ref.shape, F32)
    for q in range(pairs // c_local):
        mine = query == q
        highest = jnp.max(jnp.where(mine, score, -jnp.inf), axis=0, keepdims=True)
        expsum = jnp.sum(jnp.where(mine, jnp.exp(score - highest), 0.0), axis=0, keepdims=True)
        tsum = jnp.sum(jnp.where(mine, weight, 0.0), axis=0, keepdims=True)
        tdot = jnp.sum(jnp.where(mine, weight * score, 0.0), axis=0, keepdims=True)
        losses = jnp.where(lane == q, highest + jnp.log(expsum) - tdot / tsum, losses)
        grad = jnp.exp(own_score - highest) / expsum - jnp.exp(own_label) / tsum
        score_grad = jnp.where(own_query == q, grad, score_grad)
    loss_ref[...] = losses
    pooled = pooled_ref[...]
    sw = sw_ref[...]
    factor = lax.rsqrt(jnp.mean(pooled * pooled, axis=-1, keepdims=True) + EPS)
    inner = jnp.sum(pooled * sw, axis=-1, keepdims=True) / width
    pooled_grad = score_grad * (factor * sw - pooled * (factor * factor * factor * inner))
    out_grad = (pooled_grad / len_ref[...]).astype(BF16)
    g = dot(out_grad, wo_ref[...], NT).astype(BF16)
    g_ref[...] = g
    high, low = split2(ctx_ref[...])
    dwo_ref[...] = dot(
        jnp.concatenate([high, low], axis=0), jnp.concatenate([out_grad, out_grad], axis=0), TN
    ).astype(BF16)
    col_head = lax.broadcasted_iota(jnp.int32, g.shape, 1) // hd
    g32 = g.astype(F32)
    spread = [jnp.where(col_head == h, g32, 0.0) for h in range(heads)]
    dwv_ref[...] = dot(
        a_ref[...].astype(BF16), jnp.concatenate(spread, axis=0).astype(BF16), TN
    ).astype(BF16)


def bwd_kernel(step, heads, qkv_ref, pt_ref, g_ref, nt_ref, out_ref, acc_ref, dqt_ref, dk_ref):
    seq = pt_ref.shape[2]
    width = qkv_ref.shape[1] // 3
    hd = width // heads
    for b in range(step):
        rows = slice(b * seq, (b + 1) * seq)
        kt = qkv_ref[rows, width : 2 * width].T
        for h in range(heads):
            cols = slice(h * hd, (h + 1) * hd)
            v = qkv_ref[rows, 2 * width + h * hd : 2 * width + (h + 1) * hd]
            u = dot(v, jnp.broadcast_to(g_ref[b, 0:1, cols], (seq, hd)), NT)
            pt = pt_ref[b, h].astype(F32)
            r = jnp.sum(pt * u, axis=0, keepdims=True)
            t = (pt * (u - r)).astype(BF16)
            dk_ref[rows, cols] = dot(t, qkv_ref[rows, cols]).astype(BF16)
            dqt_ref[cols, rows] = dot(kt[cols, :], t).astype(BF16)

    @pl.when(pl.program_id(0) == 0)
    def _():
        acc_ref[...] = jnp.zeros_like(acc_ref)

    acc_ref[:, :width] += dot(nt_ref[...], dqt_ref[...], NT)
    acc_ref[:, width:] += dot(nt_ref[...], dk_ref[...])

    @pl.when(pl.program_id(0) == pl.num_programs(0) - 1)
    def _():
        out_ref[...] = acc_ref[...].astype(BF16)


VM = pl.BlockSpec(memory_space=pltpu.VMEM)


def struct(shape, dtype):
    return jax.ShapeDtypeStruct(shape, dtype)


def shards(hidden, attn_weight, norm_gain, pos_bias, score_weight, pair_lengths, labels):
    q_local, c_local, seq, width = hidden.shape
    heads = pos_bias.shape[0]
    hd = width // heads
    pairs = q_local * c_local
    group = max(1, min(heads, 256 // hd))
    while heads % group:
        group -= 1
    groups = heads // group
    gw = group * hd
    step = 4
    while pairs % step:
        step //= 2
    grid = pairs // step
    tokens = hidden.reshape(pairs, seq, width)
    lens = pair_lengths.reshape(-1)
    len_col = lens.astype(F32)[:, None]
    label_col = labels.reshape(-1).astype(F32)[:, None]
    bias_t = jnp.swapaxes(pos_bias, 1, 2)
    sw = score_weight[None, :]

    weights = lax.all_gather(attn_weight, "dp", axis=0, tiled=True)
    chunks = [
        jnp.concatenate(
            [weights[:, s * width + g * gw : s * width + (g + 1) * gw] for s in range(3)], axis=1
        )
        for g in range(groups)
    ]
    wo = weights[:, 3 * width :]

    normed, normed_t, mean = pl.pallas_call(
        functools.partial(norm_kernel, step),
        grid_spec=pltpu.PrefetchScalarGridSpec(
            num_scalar_prefetch=1,
            grid=(grid,),
            in_specs=[
                pl.BlockSpec((step, seq, width), lambda i, s: (i, 0, 0)),
                pl.BlockSpec((1, width), lambda i, s: (0, 0)),
            ],
            out_specs=[
                pl.BlockSpec((step * seq, width), lambda i, s: (i, 0)),
                pl.BlockSpec((width, step * seq), lambda i, s: (0, i)),
                pl.BlockSpec((step, 1, width), lambda i, s: (i, 0, 0)),
            ],
        ),
        out_shape=[
            struct((pairs * seq, width), BF16),
            struct((width, pairs * seq), BF16),
            struct((pairs, 1, width), F32),
        ],
        name="norm",
    )(lens, tokens, norm_gain[None, :])

    saved = []
    for g in range(groups):
        saved.append(
            pl.pallas_call(
                functools.partial(fwd_kernel, step, group),
                grid_spec=pltpu.PrefetchScalarGridSpec(
                    num_scalar_prefetch=1,
                    grid=(grid,),
                    in_specs=[
                        pl.BlockSpec((step * seq, width), lambda i, s: (i, 0)),
                        pl.BlockSpec((width, 3 * gw), lambda i, s: (0, 0)),
                        pl.BlockSpec((group, seq, seq), lambda i, s, g=g: (g, 0, 0)),
                    ],
                    out_specs=[
                        pl.BlockSpec((step * seq, 3 * gw), lambda i, s: (i, 0)),
                        pl.BlockSpec((step, group, seq, seq), lambda i, s: (i, 0, 0, 0)),
                        pl.BlockSpec((step, group, seq), lambda i, s: (i, 0, 0)),
                        pl.BlockSpec((step, 1, gw), lambda i, s: (i, 0, 0)),
                    ],
                ),
                out_shape=[
                    struct((pairs * seq, 3 * gw), BF16),
                    struct((pairs, group, seq, seq), BF16),
                    struct((pairs, group, seq), F32),
                    struct((pairs, 1, gw), F32),
                ],
                name="fwd%d" % g,
            )(lens, normed, chunks[g], bias_t)
        )

    pooled, ctx, own = pl.pallas_call(
        functools.partial(score_kernel, groups),
        in_specs=[VM] * (groups + 5),
        out_specs=[VM] * 3,
        out_shape=[
            struct((pairs, width), F32),
            struct((pairs, width), F32),
            struct((pairs, LANES), F32),
        ],
        name="score",
    )(*[s[3].reshape(pairs, gw) for s in saved], mean.reshape(pairs, width), len_col, label_col, wo, sw)

    n_cand = lax.axis_size("cand")
    everyone = [own]
    for m in range(1, n_cand):
        everyone.append(lax.ppermute(own, "cand", [(i, i ^ m) for i in range(n_cand)]))
    everyone = jnp.concatenate(everyone, axis=0)

    a = pl.pallas_call(
        functools.partial(value_kernel, groups, group),
        grid=(pairs,),
        in_specs=[pl.BlockSpec((1, group, seq), lambda i: (i, 0, 0))] * groups
        + [pl.BlockSpec((seq, width), lambda i: (i, 0))],
        out_specs=pl.BlockSpec((1, heads, width), lambda i: (i, 0, 0)),
        out_shape=struct((pairs, heads, width), F32),
        name="value",
    )(*[s[2] for s in saved], normed)
    a = jnp.swapaxes(a, 0, 1).reshape(heads * pairs, width)

    g_all, dwo, dwv, loss = pl.pallas_call(
        functools.partial(head_kernel, c_local, heads),
        in_specs=[VM] * 7,
        out_specs=[VM] * 4,
        out_shape=[
            struct((pairs, width), BF16),
            struct((width, width), BF16),
            struct((width, width), BF16),
            struct((8, LANES), F32),
        ],
        name="head",
    )(everyone, pooled, ctx, len_col, a, wo, sw)
    loss = loss[0, :q_local]

    dqk = []
    for g in range(groups):
        dqk.append(
            pl.pallas_call(
                functools.partial(bwd_kernel, step, group),
                grid=(grid,),
                in_specs=[
                    pl.BlockSpec((step * seq, 3 * gw), lambda i: (i, 0)),
                    pl.BlockSpec((step, group, seq, seq), lambda i: (i, 0, 0, 0)),
                    pl.BlockSpec((step, 1, gw), lambda i, g=g: (i, 0, g)),
                    pl.BlockSpec((width, step * seq), lambda i: (0, i)),
                ],
                out_specs=pl.BlockSpec((width, 2 * gw), lambda i: (0, 0)),
                out_shape=struct((width, 2 * gw), BF16),
                scratch_shapes=[
                    pltpu.VMEM((width, 2 * gw), F32),
                    pltpu.VMEM((gw, step * seq), BF16),
                    pltpu.VMEM((step * seq, gw), BF16),
                ],
                name="bwd%d" % g,
            )(saved[g][0], saved[g][1], g_all.reshape(pairs, 1, width), normed_t)
        )
    partial = jnp.concatenate(
        [d[:, :gw] for d in dqk] + [d[:, gw:] for d in dqk] + [dwv, dwo], axis=1
    )
    shard = lax.psum_scatter(partial, "dp", scatter_dimension=0, tiled=True)
    shard = lax.psum(shard, "cand").astype(F32)
    squares = lax.psum(jnp.sum(shard * shard), "dp")
    update = shard / (jnp.sqrt(squares / (4.0 * width * width)) + EPS)
    return (update, loss)


def solution(mesh):
    in_specs = (
        P("dp", "cand", None, None),
        P("dp", None),
        P(),
        P(),
        P(),
        P("dp", "cand"),
        P("dp", "cand"),
    )
    out_specs = (P("dp", None), P("dp"))
    return jax.shard_map(shards, mesh=mesh, in_specs=in_specs, out_specs=out_specs, check_vma=False)
```

time: 464 us -> 376 us (0.81)
  Pallas kernels: 0 us -> 98.2 us
  matrix products: 83.9 us -> 0 us
  local copies, waits for them, and re-layouts: 76.2 us -> 31.7 us
  other arithmetic: 47.1 us -> 8.8 us
  blocking collectives: 34.2 us -> 22 us
  waiting for transfers between devices: 204 us -> 198 us
    pallas_call x0 -> x10, Pallas kernels: none -> 98.2 us  [the longest x3 47 us: shards(): pl.pallas_call(functools.partial(fwd_kernel, step, group), grid_spec=pltp...]
    dot_general x11 -> x0, matrix products: 83.9 us -> none  [the longest x3 24.4 us: attend(): jnp.einsum('bhqk,bkhd->bqhd', probs, parts[:, :, 2], preferred_element_ty...]
    add_any x1 -> x0, local copies, waits for them, and re-layouts: 26.1 us -> none  [attend(): parts[:, :, 0]]
    reduce_sum x8 -> x0, other arithmetic: 24.8 us -> none  [the longest x1 10.1 us: attend(): expo = jnp.exp(logits - highest)]
    convert_element_type x3 -> x2, local copies, waits for them, and re-layouts: 19.9 us -> 1.35 us  [the longest x1 0.68 us: shards(): len_col = lens.astype(F32)[:, None]]
    add_any x2 -> x0, other arithmetic: 6.92 us -> none  [the longest x1 6.83 us: attend(): parts[:, :, 0]]
    unnamed x47 -> x24, local copies, waits for them, and re-layouts: 22.7 us -> 15.9 us
    psum x1 -> x0, blocking collectives: 6.61 us -> none  [shards(): lax.psum((jnp.sum(jnp.exp(scores - highest[:, None]), axis=1), jnp.sum(ta...]
  transfers between devices with their start and end apart: 3 -> 6, of which waited for: 3 -> 3; matrix products, arithmetic and copies ran while one was open for 2% -> 3% of each run, Pallas kernels for 0% -> 5%
where the time goes in v1:
time: 376 us; the launch traced here: 375 us
  waiting for transfers between devices  198 us (53%)
  Pallas kernels  98.2 us (26%)
  local copies, waits for them, and re-layouts  31.7 us (8%)
  blocking collectives  22 us (6%)
  between operations  14.5 us (4%)
  other arithmetic  8.8 us (2%)
    reduce_scatter x1, waiting for transfers between devices, shards(): shard = lax.psum_scatter(partial, 'dp', scatter_dimension=0, tiled=True)  94.1 us
    all_gather x1, waiting for transfers between devices, shards(): weights = lax.all_gather(attn_weight, 'dp', axis=0, tiled=True)  67.2 us
    pallas_call x3, Pallas kernels, shards(): pl.pallas_call(functools.partial(fwd_kernel, step, group), grid_spec=pltp...  47 us
    psum x1, waiting for transfers between devices, shards(): shard = lax.psum(shard, 'cand').astype(F32)  35.8 us
    pallas_call x3, Pallas kernels, shards(): pl.pallas_call(functools.partial(bwd_kernel, step, group), grid=(grid,),...  27.3 us
    psum x1, blocking collectives, shards(): squares = lax.psum(jnp.sum(shard * shard), 'dp')  22 us
    unnamed x24, local copies, waits for them, and re-layouts  15.9 us
    pallas_call x1, Pallas kernels, shards(): pl.pallas_call(functools.partial(value_kernel, groups, group), grid=(pair...  10.7 us
  transfers between devices with their start and end apart: 6, of which 3 were waited for; matrix products, arithmetic and copies ran while one was open for 3% of the time, Pallas kernels for 5%

profile of v1, /device:TPU:0, one launch (start us, length us, event | category | flops | bytes accessed | tf_op | source)
XLA Modules:
  0.0 375.0 jit_solution(2007216852864994312)
XLA Ops:
  14.5 2.3 copy.14
  16.8 6.8 %norm.1 = (bf16[2048,768]{1,0:T(8,128)(2,1)}, bf16[768,2048]{1,0:T(8,128)(2,1)}, f32[16,1,768]{2,1,0:T(1,128)}) custom-call(s32[16]{0:T(128)} %reshape.53.len_ref, bf16[16,128,768]{2,1,0:T(8,128)(2,1)} %bitcast.22, f32[1,768]{1,0:T(1,128)} %broadcast_in_dim.8.gain_ref), custom_call_target="tpu_custom_call" | custom-call | tf_op jit(solution)/shard_map/norm/pallas_call | solution.py:204
  25.0 67.2 %all-gather.2.cloned.1.call-done = bf16[768,3072]{1,0:T(8,128)(2,1)} async-done(((bf16[96,3072]{1,0:T(8,128)(2,1)}), bf16[768,3072]{1,0:T(8,128)(2,1)}) %all-gather.2.cloned.1.call-update) | async-done | bytes 4718608 | tf_op jit(solution)/shard_map/all_gather | solution.py:195
  92.2 2.2 fusion.1
  95.5 15.7 %fwd2.1 = (bf16[2048,768]{1,0:T(8,128)(2,1)}, bf16[16,4,128,128]{3,2,1,0:T(8,128)(2,1)}, f32[16,4,128]{2,1,0:T(4,128)}, f32[16,1,256]{2,1,0:T(1,128)}) custom-call(s32[16]{0:T(128)} %reshape.53.len_ref, bf16[2048,768]{1,0:T(8,128)(2,1)} %get-tuple-element.24.normed_ref.refs_3_, bf16[768,768]{1,0:T(8,128)(2,1)} %pad_maximum_fusion.2.w_ref, ...), custom_call_target="tpu_custom_call" | custom-call | tf_op jit(solution)/shard_map/fwd2/pallas_call | solution.py:230
  112.5 1.6 pad_maximum_fusion
  114.1 15.6 %fwd1.1 = (bf16[2048,768]{1,0:T(8,128)(2,1)}, bf16[16,4,128,128]{3,2,1,0:T(8,128)(2,1)}, f32[16,4,128]{2,1,0:T(4,128)}, f32[16,1,256]{2,1,0:T(1,128)}) custom-call(s32[16]{0:T(128)} %reshape.53.len_ref, bf16[2048,768]{1,0:T(8,128)(2,1)} %get-tuple-element.24.normed_ref.refs_3_, bf16[768,768]{1,0:T(8,128)(2,1)} %get-tuple-element.56.w_ref, ...), custom_call_target="tpu_custom_call" | custom-call | tf_op jit(solution)/shard_map/fwd1/pallas_call | solution.py:230
  131.1 15.7 %fwd0.1 = (bf16[2048,768]{1,0:T(8,128)(2,1)}, bf16[16,4,128,128]{3,2,1,0:T(8,128)(2,1)}, f32[16,4,128]{2,1,0:T(4,128)}, f32[16,1,256]{2,1,0:T(1,128)}) custom-call(s32[16]{0:T(128)} %reshape.53.len_ref, bf16[2048,768]{1,0:T(8,128)(2,1)} %get-tuple-element.24.normed_ref.refs_3_, bf16[768,768]{1,0:T(8,128)(2,1)} %get-tuple-element.55.w_ref, ...), custom_call_target="tpu_custom_call" | custom-call | tf_op jit(solution)/shard_map/fwd0/pallas_call | solution.py:230
  148.1 2.4 slice.77.refs_6_.wo_ref
  150.4 2.6 score.1
  153.0 1.5 collective-permute-start.1
  154.9 10.7 %value.1 = f32[16,12,768]{2,1,0:T(8,128)} custom-call(f32[16,4,128]{2,1,0:T(4,128)} %get-tuple-element.34.refs_0_, f32[16,4,128]{2,1,0:T(4,128)} %get-tuple-element.35.refs_1_, f32[16,4,128]{2,1,0:T(4,128)} %get-tuple-element.36.refs_2_, bf16[2048,768]{1,0:T(8,128)(2,1)} %get-tuple-element.24.normed_ref.refs_3_), custom_call_target="tpu_custom_call" | custom-call | tf_op jit(solution)/shard_map/value/pallas_call | solution.py:275
  165.6 2.3 copy.17
  168.5 3.9 %head.1 = (bf16[16,768]{1,0:T(8,128)(2,1)}, bf16[768,768]{1,0:T(8,128)(2,1)}, bf16[768,768]{1,0:T(8,128)(2,1)}, f32[8,128]{1,0:T(8,128)}) custom-call(f32[64,128]{1,0:T(8,128)} %pad_maximum_fusion.3.all_ref, f32[16,768]{1,0:T(8,128)} %get-tuple-element.32.pooled_ref, f32[16,768]{1,0:T(8,128)} %get-tuple-element.33.ctx_ref, ...), custom_call_target="tpu_custom_call" | custom-call | tf_op jit(solution)/shard_map/head/pallas_call | solution.py:286
  173.8 9.0 %bwd0.1 = bf16[768,512]{1,0:T(8,128)(2,1)} custom-call(bf16[2048,768]{1,0:T(8,128)(2,1)} %get-tuple-element.25.qkv_ref, bf16[16,4,128,128]{3,2,1,0:T(8,128)(2,1)} %get-tuple-element.26.pt_ref, bf16[16,1,768]{2,1,0:T(2,128)(2,1)} %copy.19.g_ref, bf16[768,2048]{1,0:T(8,128)(2,1)} %get-tuple-element.38.nt_ref), custom_call_target="tpu_custom_call" | custom-call | tf_op jit(solution)/shard_map/bwd0/pallas_call | solution.py:303
  182.8 1.8 slice_dynamic-update-slice_fusion.5
  184.6 9.0 %bwd2.1 = bf16[768,512]{1,0:T(8,128)(2,1)} custom-call(bf16[2048,768]{1,0:T(8,128)(2,1)} %get-tuple-element.41.qkv_ref, bf16[16,4,128,128]{3,2,1,0:T(8,128)(2,1)} %get-tuple-element.42.pt_ref, bf16[16,1,768]{2,1,0:T(2,128)(2,1)} %copy.19.g_ref, bf16[768,2048]{1,0:T(8,128)(2,1)} %get-tuple-element.38.nt_ref), custom_call_target="tpu_custom_call" | custom-call | tf_op jit(solution)/shard_map/bwd2/pallas_call | solution.py:303
  193.6 9.2 %bwd1.1 = bf16[768,512]{1,0:T(8,128)(2,1)} custom-call(bf16[2048,768]{1,0:T(8,128)(2,1)} %get-tuple-element.39.qkv_ref, bf16[16,4,128,128]{3,2,1,0:T(8,128)(2,1)} %get-tuple-element.40.pt_ref, bf16[16,1,768]{2,1,0:T(2,128)(2,1)} %copy.19.g_ref, bf16[768,2048]{1,0:T(8,128)(2,1)} %get-tuple-element.38.nt_ref), custom_call_target="tpu_custom_call" | custom-call | tf_op jit(solution)/shard_map/bwd1/pallas_call | solution.py:303
  202.9 2.0 slice_dynamic-update-slice_fusion.4
  210.5 94.1 %reduce-scatter.2.cloned.1.call-done = bf16[96,3072]{1,0:T(8,128)(2,1)} async-done(((bf16[768,3072]{1,0:T(8,128)(2,1)}), bf16[96,3072]{1,0:T(8,128)(2,1)}) %reduce-scatter.2.cloned.1.call-update) | async-done | bytes 589840 | tf_op jit(solution)/shard_map/reduce_scatter | solution.py:325
  304.7 35.8 %all-reduce.2.cloned.1.call-done = bf16[96,3072]{1,0:T(8,128)(2,1)} async-done(((bf16[96,3072]{1,0:T(8,128)(2,1)}), bf16[96,3072]{1,0:T(8,128)(2,1)}) %all-reduce.2.cloned.1.call-update) | async-done | bytes 589840 | tf_op jit(solution)/shard_map/psum | solution.py:326
  340.4 2.0 fusion
  343.6 22.0 %psum.15 = f32[]{:T(128)} all-reduce(f32[]{:T(128)} %fusion), channel_id=1, replica_groups=mesh['dp'=8,'cand'=4] {'dp'}, use_global_device_ids=true, to_apply=%region_3.0 | all-reduce | flops 1 | bytes 8 | tf_op jit(solution)/shard_map/psum | solution.py:327
  366.2 2.2 convert_divide_fusion
  (44 shorter events, 23.0 us)
Async XLA Ops:
  7.2 85.1 %all-gather.2.cloned.1.call-start = ((), (), s32[]{:S(2)}) async-start(), calls=%async_computation.1 | async-start | bytes 5308416 | tf_op jit(solution)/shard_map/all_gather | solution.py:195
  7.9 296.7 %reduce-scatter.2.cloned.1.call-start = ((), (), s32[]{:S(2)}) async-start(), calls=%async_computation.2 | async-start | bytes 5308416 | tf_op jit(solution)/shard_map/reduce_scatter | solution.py:325
  153.0 14.8 %collective-permute-start.2 = (f32[16,128]{1,0:T(8,128)}, f32[16,128]{1,0:T(8,128)S(1)}, u32[]{:S(2)}, u32[]{:S(2)}) collective-permute-start(f32[16,128]{1,0:T(8,128)} %get-tuple-element.31), channel_id=1, source_target_pairs={{0,3},{1,2},{2,1},{3,0},{4,7},{5,6},{6,5},{7,4},{8,11},{9,10},{10,... | collective-permute-start | bytes 24584 | tf_op jit(solution)/shard_map/ppermute | solution.py:272
  153.0 14.8 %collective-permute-start.1 = (f32[16,128]{1,0:T(8,128)}, f32[16,128]{1,0:T(8,128)S(1)}, u32[]{:S(2)}, u32[]{:S(2)}) collective-permute-start(f32[16,128]{1,0:T(8,128)} %get-tuple-element.31), channel_id=1, source_target_pairs={{0,2},{1,3},{2,0},{3,1},{4,6},{5,7},{6,4},{7,5},{8,10},{9,11},{10,... | collective-permute-start | bytes 24584 | tf_op jit(solution)/shard_map/ppermute | solution.py:272
  154.5 13.3 %collective-permute-start = (f32[16,128]{1,0:T(8,128)}, f32[16,128]{1,0:T(8,128)S(1)}, u32[]{:S(2)}, u32[]{:S(2)}) collective-permute-start(f32[16,128]{1,0:T(8,128)} %get-tuple-element.31), channel_id=1, source_target_pairs={{0,1},{1,0},{2,3},{3,2},{4,5},{5,4},{6,7},{7,6},{8,9},{9,8},{10,11... | collective-permute-start | bytes 24584 | tf_op jit(solution)/shard_map/ppermute | solution.py:272
  154.9 13.0 %copy-start.5 = (f32[16,128]{1,0:T(8,128)S(1)}, f32[16,128]{1,0:T(8,128)}, u32[]{:S(2)}) copy-start(f32[16,128]{1,0:T(8,128)} %get-tuple-element.31) | copy-start | bytes 24580
  193.6 11.2 %copy-start = (bf16[768,512]{1,0:T(8,128)(2,1)S(1)}, bf16[768,512]{1,0:T(8,128)(2,1)}, u32[]{:S(2)}) copy-start(bf16[768,512]{1,0:T(8,128)(2,1)} %bwd2.1) | copy-start | bytes 2359300
  193.6 12.0 %copy-start.1 = (bf16[768,512]{1,0:T(8,128)(2,1)S(1)}, bf16[768,512]{1,0:T(8,128)(2,1)}, u32[]{:S(2)}) copy-start(bf16[768,512]{1,0:T(8,128)(2,1)} %bwd0.1) | copy-start | bytes 2359300
  202.9 3.6 copy-start.2
  202.9 5.2 %copy-start.4 = (bf16[768,768]{1,0:T(8,128)(2,1)S(1)}, bf16[768,768]{1,0:T(8,128)(2,1)}, u32[]{:S(2)}) copy-start(bf16[768,768]{1,0:T(8,128)(2,1)} %get-tuple-element.43) | copy-start | bytes 3538948
  205.6 3.7 copy-start.3
  210.5 129.9 %all-reduce.2.cloned.1.call-start = ((), (), s32[]{:S(2)}) async-start(), calls=%async_computation.3 | async-start | bytes 1179648 | tf_op jit(solution)/shard_map/psum | solution.py:326
Sparse Core Ops, SparseCore 0:
  10.2 82.0 all-gather.1
  210.6 93.9 reduce-scatter.1
  307.0 33.3 all-reduce.1
